TPU v7x, 32 devices: a whole 2x2x4 slice. The times are simulated.
32 devices in a mesh: trial: 4 (over x, core), shard: 4 (over z), tp: 2 (over y).
Axes of the slice: x: 2, y: 2, z: 4, core: 2. Of those that a mesh axis runs over, the one named last changes fastest.
Arguments:
- weight_query: bfloat16 [10240, 4096], P(('trial', 'shard'), 'tp'), parts along dimension 0, may hold values from -0.125 to 0.125
- low_query: bfloat16 [10240, 64], P(('trial', 'shard')), parts along dimension 0, may hold values from -0.125 to 0.125
- high_query: bfloat16 [256, 4096], P('trial', 'tp'), parts along dimension 0, may hold values from -0.75 to 0.75
- weight_key: bfloat16 [10240, 1024], P(('trial', 'shard'), 'tp'), parts along dimension 0, may hold values from -0.125 to 0.125
- low_key: bfloat16 [10240, 64], P(('trial', 'shard')), parts along dimension 0, may hold values from -0.125 to 0.125
- high_key: bfloat16 [256, 1024], P('trial', 'tp'), parts along dimension 0, may hold values from -0.75 to 0.75
- weight_value: bfloat16 [10240, 1024], P(('trial', 'shard'), 'tp'), parts along dimension 0, may hold values from -0.125 to 0.125
- low_value: bfloat16 [10240, 64], P(('trial', 'shard')), parts along dimension 0, may hold values from -0.125 to 0.125
- high_value: bfloat16 [256, 1024], P('trial', 'tp'), parts along dimension 0, may hold values from -0.75 to 0.75
- norm_train: float32 [10240], P(('trial', 'shard', 'tp')), parts along dimension 0, may hold values from 0.25 to 1.75
- norm_step: float32 [10240], P(('trial', 'shard', 'tp')), parts along dimension 0, may hold values from -0.3 to 0.3
Outputs:
- serve_query: bfloat16 [16384, 2560], P(('trial', 'tp')), parts along dimension 0
- serve_key: bfloat16 [4096, 2560], P(('trial', 'tp')), parts along dimension 0
- serve_value: bfloat16 [4096, 2560], P(('trial', 'tp')), parts along dimension 0
- serve_norm: bfloat16 [10240], P('trial'), parts along dimension 0
There are 4 independent parts, one for each index of `trial`. A program takes and returns all parts, laid end to end along the dimension named above; each array names one. Nothing has to cross between parts.
All inputs are finite; a program needn't handle non-finite values.
Results may differ from a plain program's by a relative error of at most 0.001.
Values may be sent and summed in bfloat16 or wider, within the bound.
A program may use at most 128 MiB of HBM per device.

v0:
```python
import jax
import jax.numpy as jnp
from jax import lax
from jax.sharding import PartitionSpec as P

mix_rate = 1.0


def on_device(
    weight_query,
    low_query,
    high_query,
    weight_key,
    low_key,
    high_key,
    weight_value,
    low_value,
    high_value,
    norm_train,
    norm_step,
):
    fresh_query = weight_query.astype(jnp.float32) + mix_rate * jnp.dot(
        low_query, high_query, preferred_element_type=jnp.float32
    )
    fresh_key = weight_key.astype(jnp.float32) + mix_rate * jnp.dot(
        low_key, high_key, preferred_element_type=jnp.float32
    )
    fresh_value = weight_value.astype(jnp.float32) + mix_rate * jnp.dot(
        low_value, high_value, preferred_element_type=jnp.float32
    )
    narrow_query, narrow_key, narrow_value = (
        fresh_query.astype(jnp.bfloat16),
        fresh_key.astype(jnp.bfloat16),
        fresh_value.astype(jnp.bfloat16),
    )
    serve_query, serve_key, serve_value = (
        lax.all_gather(narrow_query, "shard", axis=0, tiled=True),
        lax.all_gather(narrow_key, "shard", axis=0, tiled=True),
        lax.all_gather(narrow_value, "shard", axis=0, tiled=True),
    )
    serve_query, serve_key, serve_value = (serve_query.T, serve_key.T, serve_value.T)
    serve_norm = lax.all_gather(
        (norm_train + norm_step).astype(jnp.bfloat16), ("shard", "tp"), axis=0, tiled=True
    )
    return (serve_query, serve_key, serve_value, serve_norm)


def solution(mesh):
    in_specs = (
        P(("trial", "shard"), "tp"),
        P(("trial", "shard"), None),
        P("trial", "tp"),
        P(("trial", "shard"), "tp"),
        P(("trial", "shard"), None),
        P("trial", "tp"),
        P(("trial", "shard"), "tp"),
        P(("trial", "shard"), None),
        P("trial", "tp"),
        P(("trial", "shard", "tp")),
        P(("trial", "shard", "tp")),
    )
    out_specs = (
        P(("trial", "tp"), None),
        P(("trial", "tp"), None),
        P(("trial", "tp"), None),
        P("trial"),
    )
    return jax.shard_map(
        on_device, mesh=mesh, in_specs=in_specs, out_specs=out_specs, check_vma=False
    )
```

profile of v0, /device:TPU:16, one launch (start us, length us, event | category | flops | bytes accessed | tf_op | source)
XLA Modules:
  0.0 325.0 jit_solution(5912518785013301905)
XLA Ops:
  7.2 0.0 copy-start
  7.2 0.0 copy-start.1
  7.2 0.0 copy-start.2
  7.2 0.0 all-gather.6.cloned.1.call-start
  7.2 2.5 fusion
  9.7 0.0 all-gather.6.cloned.1.call-update
  9.8 0.0 all-gather.8.cloned.1.call-start
  9.8 2.4 fusion.1
  12.2 0.0 all-gather.8.cloned.1.call-update
  12.2 0.0 all-gather.4.cloned.1.call-start
  12.3 0.0 copy-done
  12.3 0.0 copy-done.1
  12.3 0.0 copy-done.2
  12.3 2.4 add_convert_fusion
  14.7 0.0 copy-start.5
  14.7 0.0 copy-start.3
  14.7 0.0 copy-start.4
  14.7 0.0 all-gather.4.cloned.1.call-update
  14.7 0.6 copy-done.5
  15.3 0.6 dynamic-slice
  16.6 0.0 copy-done.3
  16.6 0.0 copy-done.4
  16.6 0.3 dynamic-update-slice
  16.9 19.5 %all-reduce = bf16[2560]{0:T(1024)(128)(2,1)} all-reduce(bf16[2560]{0:T(1024)(128)(2,1)S(1)} %dynamic-update-slice), channel_id=1, replica_groups=mesh['trial'=4,'shard'=4,'tp'=2] {'shard','tp'}, use_global_device_ids=true, to_apply=%add | all-reduce | flops 2560 | bytes 10240
  36.4 28.8 %all-gather.6.cloned.1.call-done = bf16[2560,512]{1,0:T(8,128)(2,1)} async-done(((bf16[640,512]{1,0:T(8,128)(2,1)}), bf16[2560,512]{1,0:T(8,128)(2,1)}) %all-gather.6.cloned.1.call-update) | async-done | bytes 2621456 | tf_op jit(solution)/shard_map/all_gather | solution.py:38
  65.2 4.4 %copy.16 = bf16[512,2560]{1,0:T(8,128)(2,1)} copy(bf16[512,2560]{0,1:T(8,128)(2,1)} %bitcast.11) | data formatting | bytes 5242880
  69.5 51.0 %all-gather.8.cloned.1.call-done = bf16[2560,512]{1,0:T(8,128)(2,1)} async-done(((bf16[640,512]{1,0:T(8,128)(2,1)}), bf16[2560,512]{1,0:T(8,128)(2,1)}) %all-gather.8.cloned.1.call-update) | async-done | bytes 2621456 | tf_op jit(solution)/shard_map/all_gather | solution.py:39
  120.5 4.4 %copy.17 = bf16[512,2560]{1,0:T(8,128)(2,1)} copy(bf16[512,2560]{0,1:T(8,128)(2,1)} %bitcast.12) | data formatting | bytes 5242880
  124.9 179.9 %all-gather.4.cloned.1.call-done = bf16[2560,2048]{1,0:T(8,128)(2,1)} async-done(((bf16[640,2048]{1,0:T(8,128)(2,1)}), bf16[2560,2048]{1,0:T(8,128)(2,1)}) %all-gather.4.cloned.1.call-update) | async-done | bytes 10485776 | tf_op jit(solution)/shard_map/all_gather | solution.py:37
  304.8 13.7 %copy.15 = bf16[2048,2560]{1,0:T(8,128)(2,1)} copy(bf16[2048,2560]{0,1:T(8,128)(2,1)} %bitcast.10) | data formatting | bytes 20971520
  (2 shorter events, 0.0 us)
Async XLA Ops:
  7.2 5.1 %copy-start = (bf16[64,2048]{1,0:T(8,128)(2,1)S(1)}, bf16[64,2048]{1,0:T(8,128)(2,1)}, u32[]{:S(2)}) copy-start(bf16[64,2048]{1,0:T(8,128)(2,1)} %param.13) | copy-start | bytes 786436
  7.2 5.1 %copy-start.1 = (bf16[640,2048]{1,0:T(8,128)(2,1)S(1)}, bf16[640,2048]{1,0:T(8,128)(2,1)}, u32[]{:S(2)}) copy-start(bf16[640,2048]{1,0:T(8,128)(2,1)} %param.11) | copy-start | bytes 7864324
  7.2 5.1 %copy-start.2 = (bf16[640,64]{0,1:T(8,128)(2,1)S(1)}, bf16[640,64]{0,1:T(8,128)(2,1)}, u32[]{:S(2)}) copy-start(bf16[640,64]{0,1:T(8,128)(2,1)} %param.12) | copy-start | bytes 245764
  7.2 58.0 %all-gather.6.cloned.1.call-start = ((), (), s32[]{:S(2)}) async-start(), calls=%async_computation.1 | async-start | bytes 3276800 | tf_op jit(solution)/shard_map/all_gather | solution.py:38
  9.8 110.7 %all-gather.8.cloned.1.call-start = ((), (), s32[]{:S(2)}) async-start(), calls=%async_computation.2 | async-start | bytes 3276800 | tf_op jit(solution)/shard_map/all_gather | solution.py:39
  12.2 292.5 %all-gather.4.cloned.1.call-start = ((), (), s32[]{:S(2)}) async-start(), calls=%async_computation | async-start | bytes 13107200 | tf_op jit(solution)/shard_map/all_gather | solution.py:37
  14.7 0.7 copy-start.5
  14.7 1.9 copy-start.3
  14.7 1.9 copy-start.4
Sparse Core Ops, SparseCore 0:
  10.2 54.9 all-gather.5
  66.7 53.7 all-gather.7
  122.7 182.0 all-gather.3
where the time goes:
time: 329 us; the launch traced here: 325 us
  waiting for transfers between devices  260 us (79%)
  local copies, waits for them, and re-layouts  23.9 us (7%)
  blocking collectives  19.5 us (6%)
  between operations  14.5 us (4%)
  matrix products  7.24 us (2%)
    all_gather x1, waiting for transfers between devices, on_device(): lax.all_gather(narrow_query, 'shard', axis=0, tiled=True)  180 us
    all_gather x1, waiting for transfers between devices, on_device(): lax.all_gather(narrow_value, 'shard', axis=0, tiled=True)  51 us
    all_gather x1, waiting for transfers between devices, on_device(): lax.all_gather(narrow_key, 'shard', axis=0, tiled=True)  28.8 us
    unnamed x18, local copies, waits for them, and re-layouts  23.9 us
    unnamed x1, blocking collectives  19.5 us
  transfers between devices with their start and end apart: 3, of which 3 were waited for; matrix products, arithmetic and copies ran while one was open for 4% of the time, Pallas kernels for 0%

commit v1 on v0

v1 whole, which is shorter than its diff:
```python
import functools

import jax
import jax.numpy as jnp
from jax import lax
from jax.experimental import pallas as pl
from jax.experimental.pallas import tpu as pltpu
from jax.sharding import PartitionSpec as P

mix_rate = 1.0
MESH = pl.DeviceIdType.MESH
IN_VMEM = True


def chunk_rows(widths):
    for rows in (256, 128):
        if all(width % rows == 0 for width in widths):
            return rows
    return None


def gather_kernel(n, tp, rows, *refs):
    weights, low_refs, high_refs = refs[0:3], refs[3:6], refs[6:9]
    norm_ref = refs[9]
    outs = refs[10:13]
    norm_out = refs[13]
    staged, lows, highs = refs[14], refs[15:18], refs[18:21]
    norm_all, load_sem, small_sem, send_sem, recv_sem, norm_send, norm_recv = refs[21:]
    me, my_tp = lax.axis_index("shard"), lax.axis_index("tp")
    right = lax.rem(me + 1, n)
    depth = staged.shape[1]
    counts = [weight.shape[1] // rows for weight in weights]
    starts = [sum(counts[:i]) for i in range(len(counts))]
    total = sum(counts)

    def load(which, c):
        return pltpu.make_async_copy(
            weights[which].at[:, pl.ds(pl.multiple_of(c * rows, rows), rows)],
            staged.at[starts[which] + c],
            load_sem.at[starts[which] + c],
        )

    small = [
        (
            pltpu.make_async_copy(low_refs[i], lows[i], small_sem.at[2 * i]),
            pltpu.make_async_copy(high_refs[i], highs[i], small_sem.at[2 * i + 1]),
        )
        for i in range(3)
    ]
    for which in range(3):
        for copy in small[which]:
            copy.start()

        @pl.loop(0, counts[which])
        def _(c):
            load(which, c).start()

    partners = [(k, t) for k in range(n) for t in range(tp) if (k, t) != (0, 0)]

    def partner(k, t):
        return {"shard": lax.rem(me + k, n), "tp": lax.rem(my_tp + t, tp)}

    barrier = pltpu.get_barrier_semaphore()
    for k, t in partners:
        pl.semaphore_signal(barrier, inc=1, device_id=partner(k, t), device_id_type=MESH)
    pl.semaphore_wait(barrier, len(partners))

    def block(which, c, owner):
        return outs[which].at[
            pl.ds(pl.multiple_of(c * rows, rows), rows),
            pl.ds(pl.multiple_of(owner * depth, 128), depth),
        ]

    def send(which, c, step):
        here = block(which, c, lax.rem(me - step + n, n))
        slot = step * total + starts[which] + c
        return pltpu.make_async_remote_copy(
            here, here, send_sem.at[slot], recv_sem.at[slot],
            device_id={"shard": right}, device_id_type=MESH,
        )

    def arrival(which, c, step):
        here = block(which, c, lax.rem(me - step - 1 + n, n))
        slot = step * total + starts[which] + c
        return pltpu.make_async_remote_copy(
            here, here, send_sem.at[slot], recv_sem.at[slot],
            device_id={"shard": right}, device_id_type=MESH,
        )

    for which in range(3):
        for copy in small[which]:
            copy.wait()

        @pl.loop(0, counts[which])
        def _(c):
            load(which, c).wait()
            high = highs[which][:, pl.ds(pl.multiple_of(c * rows, rows), rows)]
            fresh = staged[starts[which] + c].astype(jnp.float32) + mix_rate * lax.dot_general(
                lows[which][...], high, (((0,), (0,)), ((), ())),
                preferred_element_type=jnp.float32,
            )
            outs[which][
                pl.ds(pl.multiple_of(c * rows, rows), rows),
                pl.ds(pl.multiple_of(me * depth, 128), depth),
            ] = fresh.astype(jnp.bfloat16).T
            send(which, c, 0).start()

    def norm_copy(i, k, t):
        mine = me * tp + my_tp
        return pltpu.make_async_remote_copy(
            norm_ref, norm_all.at[mine], norm_send.at[i], norm_recv.at[i],
            device_id=partner(k, t), device_id_type=MESH,
        )

    def norm_arrival(i, k, t):
        theirs = lax.rem(me - k + n, n) * tp + lax.rem(my_tp - t + tp, tp)
        return pltpu.make_async_remote_copy(
            norm_ref, norm_all.at[theirs], norm_send.at[i], norm_recv.at[i],
            device_id=partner(k, t), device_id_type=MESH,
        )

    for i, (k, t) in enumerate(partners):
        norm_copy(i, k, t).start()
    norm_all[me * tp + my_tp] = norm_ref[...]

    for step in range(n - 1):
        for which in range(3):

            @pl.loop(0, counts[which])
            def _(c):
                arrival(which, c, step).wait_recv()
                if step < n - 2:
                    send(which, c, step + 1).start()

        if step == 0:
            for i, (k, t) in enumerate(partners):
                norm_arrival(i, k, t).wait_recv()
            norm_out[...] = norm_all[...].astype(jnp.bfloat16)

    for step in range(n - 1):
        for which in range(3):

            @pl.loop(0, counts[which])
            def _(c):
                send(which, c, step).wait_send()

    for i, (k, t) in enumerate(partners):
        norm_copy(i, k, t).wait_send()


def gathered(n, tp, rows, weights, lows, highs, norm):
    depth = weights[0].shape[0]
    total = sum(weight.shape[1] // rows for weight in weights)
    group, part = n * tp, norm.shape[1]
    make = pltpu.VMEM if IN_VMEM else jax.ShapeDtypeStruct
    space = pl.BlockSpec(memory_space=pltpu.VMEM if IN_VMEM else pl.ANY)
    vmem, hbm = pl.BlockSpec(memory_space=pltpu.VMEM), pl.BlockSpec(memory_space=pltpu.HBM)
    return pl.pallas_call(
        functools.partial(gather_kernel, n, tp, rows),
        out_shape=[make((weight.shape[1], n * depth), jnp.bfloat16) for weight in weights]
        + [jax.ShapeDtypeStruct((group, 1, part), jnp.bfloat16)],
        in_specs=[hbm] * 9 + [vmem],
        out_specs=[space] * 3 + [vmem],
        scratch_shapes=[
            pltpu.VMEM((total, depth, rows), jnp.bfloat16),
            *[pltpu.VMEM(x.shape, x.dtype) for x in (*lows, *highs)],
            pltpu.VMEM((group, 1, part), jnp.float32),
            pltpu.SemaphoreType.DMA((total,)),
            pltpu.SemaphoreType.DMA((6,)),
            pltpu.SemaphoreType.DMA(((n - 1) * total,)),
            pltpu.SemaphoreType.DMA(((n - 1) * total,)),
            pltpu.SemaphoreType.DMA((group - 1,)),
            pltpu.SemaphoreType.DMA((group - 1,)),
        ],
        compiler_params=pltpu.CompilerParams(
            collective_id=0, has_side_effects=True, vmem_limit_bytes=47 * 2**20
        ),
    )(*weights, *lows, *highs, norm)


def flush_kernel(count, *refs):
    sources, results, sems = refs[:count], refs[count : 2 * count], refs[-1]
    copies = [
        pltpu.make_async_copy(source, result, sems.at[i])
        for i, (source, result) in enumerate(zip(sources, results))
    ]
    for copy in copies:
        copy.start()
    for copy in copies:
        copy.wait()


def flushed(held):
    return pl.pallas_call(
        functools.partial(flush_kernel, len(held)),
        out_shape=[jax.ShapeDtypeStruct(x.shape, x.dtype) for x in held],
        in_specs=[pl.BlockSpec(memory_space=pltpu.VMEM)] * len(held),
        out_specs=[pl.BlockSpec(memory_space=pltpu.HBM)] * len(held),
        scratch_shapes=[pltpu.SemaphoreType.DMA((len(held),))],
        compiler_params=pltpu.CompilerParams(vmem_limit_bytes=2**20),
    )(*held)


def plain(weights, lows, highs, norm_new):
    serve = []
    for weight, low, high in zip(weights, lows, highs):
        fresh = weight.astype(jnp.float32) + mix_rate * jnp.dot(
            low, high, preferred_element_type=jnp.float32
        )
        serve.append(
            lax.all_gather(fresh.astype(jnp.bfloat16), "shard", axis=0, tiled=True).T
        )
    norm = lax.all_gather(
        norm_new.astype(jnp.bfloat16), ("shard", "tp"), axis=0, tiled=True
    )
    return (*serve, norm)


def on_device(n, tp, wq, lq, hq, wk, lk, hk, wv, lv, hv, norm_train, norm_step):
    weights, lows, highs = (wq, wk, wv), (lq, lk, lv), (hq, hk, hv)
    rows = chunk_rows([weight.shape[1] for weight in weights])
    norm_new = norm_train + norm_step
    if n < 2 or rows is None or wq.shape[0] % 128:
        return plain(weights, lows, highs, norm_new)
    *serve, norm = gathered(
        n, tp, rows, weights, [low.T for low in lows], highs, norm_new.reshape(1, -1)
    )
    return (*flushed(serve), norm.reshape(-1))


def solution(mesh):
    in_specs = (
        (P(("trial", "shard"), "tp"), P(("trial", "shard"), None), P("trial", "tp")) * 3
        + (P(("trial", "shard", "tp")),) * 2
    )
    out_specs = (P(("trial", "tp"), None),) * 3 + (P("trial"),)
    body = functools.partial(on_device, mesh.shape["shard"], mesh.shape["tp"])
    return jax.shard_map(
        body, mesh=mesh, in_specs=in_specs, out_specs=out_specs, check_vma=False
    )
```

time: 329 us -> 314 us (0.954); the launches traced: 325 us -> 314 us
  Pallas kernels: 0 us -> 311 us
  waiting for transfers between devices: 260 us -> 0 us
  local copies, waits for them, and re-layouts: 23.9 us -> 1.25 us
  blocking collectives: 19.5 us -> 0 us
  between operations: 14.5 us -> 0.67 us
  matrix products: 7.24 us -> 0 us
    pallas_call x0 -> x2, Pallas kernels: none -> 311 us  [the longest x1 305 us: gathered(): pl.pallas_call(functools.partial(gather_kernel, n, tp, rows), out_shape=[...]
    all_gather x3 -> x0, waiting for transfers between devices: 260 us -> none  [the longest x1 180 us: on_device(): lax.all_gather(narrow_query, 'shard', axis=0, tiled=True)]
    unnamed x18 -> x2, local copies, waits for them, and re-layouts: 23.9 us -> 0.01 us
    unnamed x1 -> x0, blocking collectives: 19.5 us -> none
    dot_general x3 -> x0, matrix products: 7.24 us -> none  [the longest x1 2.5 us: on_device(): jnp.dot(low_key, high_key, preferred_element_type=jnp.float32)]
  transfers between devices with their start and end apart: 3 -> 0, of which waited for: 3 -> 0; matrix products, arithmetic and copies ran while one was open for 4% -> 0% of each run, Pallas kernels for 0% -> 0%
where the time goes in v1:
time: 314 us
  Pallas kernels  311 us (99%)
    pallas_call x1, Pallas kernels, gathered(): pl.pallas_call(functools.partial(gather_kernel, n, tp, rows), out_shape=[...  305 us

profile of v1, /device:TPU:16, one launch (start us, length us, event | category | flops | bytes accessed | tf_op | source)
XLA Modules:
  0.0 313.7 jit_solution(1397268225629620110)
XLA Ops:
  0.6 0.7 add.3
  1.3 0.6 reshape.14.refs_9_
  1.9 305.3 %shard_map.138 = (bf16[2048,2560]{1,0:T(8,128)(2,1)S(1)}, bf16[512,2560]{1,0:T(8,128)(2,1)S(1)}, bf16[512,2560]{1,0:T(8,128)(2,1)S(1)}, bf16[8,1,320]{2,1,0:T(2,128)(2,1)}) custom-call(bf16[640,2048]{1,0:T(8,128)(2,1)} %refs_0_.1, bf16[640,512]{1,0:T(8,128)(2,1)} %refs_1_.1, bf16[640,512]{1,0:T(8,128)(2,1)} %refs_2_.1, bf16[64,640]{1,0:T(8,128)(2,1)} %bitcast.3, ...), custom_call_target="tpu_custom_call" | custom-call | tf_op jit(solution)/shard_map/pallas_call | solution.py:158
  307.2 0.0 copy-start
  307.2 5.8 %shard_map.139 = (bf16[2048,2560]{1,0:T(8,128)(2,1)}, bf16[512,2560]{1,0:T(8,128)(2,1)}, bf16[512,2560]{1,0:T(8,128)(2,1)}) custom-call(bf16[2048,2560]{1,0:T(8,128)(2,1)S(1)} %get-tuple-element.11.refs_0_, bf16[512,2560]{1,0:T(8,128)(2,1)S(1)} %get-tuple-element.12.refs_1_, bf16[512,2560]{1,0:T(8,128)(2,1)S(1)} %get-tuple-element.13.refs_2_), custom_call_target="tpu_custom_call" | custom-call | tf_op jit(solution)/shard_map/pallas_call | solution.py:194
  313.0 0.0 copy-done
  313.0 0.7 reshape.15
  (1 shorter events, 0.0 us)
Async XLA Ops:
  307.2 5.8 %copy-start = (bf16[8,1,320]{2,1,0:T(2,128)(2,1)S(1)}, bf16[8,1,320]{2,1,0:T(2,128)(2,1)}, u32[]{:S(2)}) copy-start(bf16[8,1,320]{2,1,0:T(2,128)(2,1)} %get-tuple-element.17) | copy-start | bytes 15364

commit v2 on v1

--- a/solution.py
+++ b/solution.py
@@ -27,7 +27,6 @@
     staged, lows, highs = refs[14], refs[15:18], refs[18:21]
     norm_all, load_sem, small_sem, send_sem, recv_sem, norm_send, norm_recv = refs[21:]
     me, my_tp = lax.axis_index("shard"), lax.axis_index("tp")
-    right = lax.rem(me + 1, n)
     depth = staged.shape[1]
     counts = [weight.shape[1] // rows for weight in weights]
     starts = [sum(counts[:i]) for i in range(len(counts))]
@@ -71,21 +70,27 @@
             pl.ds(pl.multiple_of(owner * depth, 128), depth),
         ]
 
-    def send(which, c, step):
-        here = block(which, c, lax.rem(me - step + n, n))
-        slot = step * total + starts[which] + c
+    def hop(which, c, step, way, owner):
+        here = block(which, c, owner)
+        slot = ((0 if way > 0 else 1) * (n - 1) + step) * total + starts[which] + c
         return pltpu.make_async_remote_copy(
             here, here, send_sem.at[slot], recv_sem.at[slot],
-            device_id={"shard": right}, device_id_type=MESH,
-        )
-
-    def arrival(which, c, step):
-        here = block(which, c, lax.rem(me - step - 1 + n, n))
-        slot = step * total + starts[which] + c
-        return pltpu.make_async_remote_copy(
-            here, here, send_sem.at[slot], recv_sem.at[slot],
-            device_id={"shard": right}, device_id_type=MESH,
-        )
+            device_id={"shard": jnp.clip(me + way, 0, n - 1)}, device_id_type=MESH,
+        )
+
+    def sends(step, way):
+        owner = me - way * step
+        ok = (owner >= 0) & (owner < n) & (me + way >= 0) & (me + way < n)
+        return ok, jnp.clip(owner, 0, n - 1)
+
+    def arrives(step, way):
+        owner = me - way * (step + 1)
+        return (owner >= 0) & (owner < n), jnp.clip(owner, 0, n - 1)
+
+    def send(which, c, step):
+        for way in (1, -1):
+            ok, owner = sends(step, way)
+            pl.when(ok)(lambda: hop(which, c, step, way, owner).start())
 
     for which in range(3):
         for copy in small[which]:
@@ -103,7 +108,7 @@
                 pl.ds(pl.multiple_of(c * rows, rows), rows),
                 pl.ds(pl.multiple_of(me * depth, 128), depth),
             ] = fresh.astype(jnp.bfloat16).T
-            send(which, c, 0).start()
+            send(which, c, 0)
 
     def norm_copy(i, k, t):
         mine = me * tp + my_tp
@@ -123,26 +128,31 @@
         norm_copy(i, k, t).start()
     norm_all[me * tp + my_tp] = norm_ref[...]
 
+    def pass_on(which, c, step):
+        for way in (1, -1):
+            ok, owner = arrives(step, way)
+            further = ok & (me + way >= 0) & (me + way < n)
+            pl.when(ok)(lambda: hop(which, c, step, way, owner).wait_recv())
+            if step < n - 2:
+                pl.when(further)(lambda: hop(which, c, step + 1, way, owner).start())
+
     for step in range(n - 1):
         for which in range(3):
-
-            @pl.loop(0, counts[which])
-            def _(c):
-                arrival(which, c, step).wait_recv()
-                if step < n - 2:
-                    send(which, c, step + 1).start()
+            pl.loop(0, counts[which])(functools.partial(pass_on, which, step=step))
 
         if step == 0:
             for i, (k, t) in enumerate(partners):
                 norm_arrival(i, k, t).wait_recv()
             norm_out[...] = norm_all[...].astype(jnp.bfloat16)
 
+    def sent(which, c, step):
+        for way in (1, -1):
+            ok, owner = sends(step, way)
+            pl.when(ok)(lambda: hop(which, c, step, way, owner).wait_send())
+
     for step in range(n - 1):
         for which in range(3):
-
-            @pl.loop(0, counts[which])
-            def _(c):
-                send(which, c, step).wait_send()
+            pl.loop(0, counts[which])(functools.partial(sent, which, step=step))
 
     for i, (k, t) in enumerate(partners):
         norm_copy(i, k, t).wait_send()
@@ -167,8 +177,8 @@
             pltpu.VMEM((group, 1, part), jnp.float32),
             pltpu.SemaphoreType.DMA((total,)),
             pltpu.SemaphoreType.DMA((6,)),
-            pltpu.SemaphoreType.DMA(((n - 1) * total,)),
-            pltpu.SemaphoreType.DMA(((n - 1) * total,)),
+            pltpu.SemaphoreType.DMA((2 * (n - 1) * total,)),
+            pltpu.SemaphoreType.DMA((2 * (n - 1) * total,)),
             pltpu.SemaphoreType.DMA((group - 1,)),
             pltpu.SemaphoreType.DMA((group - 1,)),
         ],

time: 314 us -> 272 us (0.87); the launches traced: 314 us -> 267 us
  Pallas kernels: 311 us -> 265 us
    pallas_call x1, Pallas kernels: 305 us -> 259 us  [gathered(): pl.pallas_call(functools.partial(gather_kernel, n, tp, rows), out_shape=[...]
where the time goes in v2:
time: 272 us; the launch traced here: 267 us
  Pallas kernels  265 us (97%)
    pallas_call x1, Pallas kernels, gathered(): pl.pallas_call(functools.partial(gather_kernel, n, tp, rows), out_shape=[...  259 us
    pallas_call x1, Pallas kernels, flushed(): pl.pallas_call(functools.partial(flush_kernel, len(held)), out_shape=[jax...  5.76 us

profile of v2, /device:TPU:16, one launch (start us, length us, event | category | flops | bytes accessed | tf_op | source)
XLA Modules:
  0.0 267.2 jit_solution(12548726900188966245)
XLA Ops:
  0.6 0.7 add.3
  1.3 0.6 reshape.14.refs_9_
  1.9 258.8 %shard_map.138 = (bf16[2048,2560]{1,0:T(8,128)(2,1)S(1)}, bf16[512,2560]{1,0:T(8,128)(2,1)S(1)}, bf16[512,2560]{1,0:T(8,128)(2,1)S(1)}, bf16[8,1,320]{2,1,0:T(2,128)(2,1)}) custom-call(bf16[640,2048]{1,0:T(8,128)(2,1)} %refs_0_.1, bf16[640,512]{1,0:T(8,128)(2,1)} %refs_1_.1, bf16[640,512]{1,0:T(8,128)(2,1)} %refs_2_.1, bf16[64,640]{1,0:T(8,128)(2,1)} %bitcast.3, ...), custom_call_target="tpu_custom_call" | custom-call | tf_op jit(solution)/shard_map/pallas_call | solution.py:168
  260.7 0.0 copy-start
  260.7 5.8 %shard_map.139 = (bf16[2048,2560]{1,0:T(8,128)(2,1)}, bf16[512,2560]{1,0:T(8,128)(2,1)}, bf16[512,2560]{1,0:T(8,128)(2,1)}) custom-call(bf16[2048,2560]{1,0:T(8,128)(2,1)S(1)} %get-tuple-element.11.refs_0_, bf16[512,2560]{1,0:T(8,128)(2,1)S(1)} %get-tuple-element.12.refs_1_, bf16[512,2560]{1,0:T(8,128)(2,1)S(1)} %get-tuple-element.13.refs_2_), custom_call_target="tpu_custom_call" | custom-call | tf_op jit(solution)/shard_map/pallas_call | solution.py:204
  266.5 0.0 copy-done
  266.5 0.7 reshape.15
  (1 shorter events, 0.0 us)
Async XLA Ops:
  260.7 5.8 %copy-start = (bf16[8,1,320]{2,1,0:T(2,128)(2,1)S(1)}, bf16[8,1,320]{2,1,0:T(2,128)(2,1)}, u32[]{:S(2)}) copy-start(bf16[8,1,320]{2,1,0:T(2,128)(2,1)} %get-tuple-element.17) | copy-start | bytes 15364

commit v3 on v2

--- a/solution.py
+++ b/solution.py
@@ -21,11 +21,11 @@
 
 def gather_kernel(n, tp, rows, *refs):
     weights, low_refs, high_refs = refs[0:3], refs[3:6], refs[6:9]
-    norm_ref = refs[9]
-    outs = refs[10:13]
-    norm_out = refs[13]
-    staged, lows, highs = refs[14], refs[15:18], refs[18:21]
-    norm_all, load_sem, small_sem, send_sem, recv_sem, norm_send, norm_recv = refs[21:]
+    norm_train, norm_step = refs[9:11]
+    outs = refs[11:14]
+    norm_out = refs[14]
+    staged, lows, highs = refs[15], refs[16:19], refs[19:22]
+    norm_all, load_sem, small_sem, send_sem, recv_sem, norm_send, norm_recv, norm_ref = refs[22:]
     me, my_tp = lax.axis_index("shard"), lax.axis_index("tp")
     depth = staged.shape[1]
     counts = [weight.shape[1] // rows for weight in weights]
@@ -59,6 +59,7 @@
     def partner(k, t):
         return {"shard": lax.rem(me + k, n), "tp": lax.rem(my_tp + t, tp)}
 
+    norm_ref[0, :] = norm_train[...] + norm_step[...]
     barrier = pltpu.get_barrier_semaphore()
     for k, t in partners:
         pl.semaphore_signal(barrier, inc=1, device_id=partner(k, t), device_id_type=MESH)
@@ -158,10 +159,10 @@
         norm_copy(i, k, t).wait_send()
 
 
-def gathered(n, tp, rows, weights, lows, highs, norm):
+def gathered(n, tp, rows, weights, lows, highs, train, step):
     depth = weights[0].shape[0]
     total = sum(weight.shape[1] // rows for weight in weights)
-    group, part = n * tp, norm.shape[1]
+    group, part = n * tp, train.shape[0]
     make = pltpu.VMEM if IN_VMEM else jax.ShapeDtypeStruct
     space = pl.BlockSpec(memory_space=pltpu.VMEM if IN_VMEM else pl.ANY)
     vmem, hbm = pl.BlockSpec(memory_space=pltpu.VMEM), pl.BlockSpec(memory_space=pltpu.HBM)
@@ -169,7 +170,7 @@
         functools.partial(gather_kernel, n, tp, rows),
         out_shape=[make((weight.shape[1], n * depth), jnp.bfloat16) for weight in weights]
         + [jax.ShapeDtypeStruct((group, 1, part), jnp.bfloat16)],
-        in_specs=[hbm] * 9 + [vmem],
+        in_specs=[hbm] * 9 + [vmem] * 2,
         out_specs=[space] * 3 + [vmem],
         scratch_shapes=[
             pltpu.VMEM((total, depth, rows), jnp.bfloat16),
@@ -181,11 +182,12 @@
             pltpu.SemaphoreType.DMA((2 * (n - 1) * total,)),
             pltpu.SemaphoreType.DMA((group - 1,)),
             pltpu.SemaphoreType.DMA((group - 1,)),
+            pltpu.VMEM((1, part), jnp.float32),
         ],
         compiler_params=pltpu.CompilerParams(
             collective_id=0, has_side_effects=True, vmem_limit_bytes=47 * 2**20
         ),
-    )(*weights, *lows, *highs, norm)
+    )(*weights, *lows, *highs, train, step)
 
 
 def flush_kernel(count, *refs):
@@ -229,11 +231,10 @@
 def on_device(n, tp, wq, lq, hq, wk, lk, hk, wv, lv, hv, norm_train, norm_step):
     weights, lows, highs = (wq, wk, wv), (lq, lk, lv), (hq, hk, hv)
     rows = chunk_rows([weight.shape[1] for weight in weights])
-    norm_new = norm_train + norm_step
     if n < 2 or rows is None or wq.shape[0] % 128:
-        return plain(weights, lows, highs, norm_new)
+        return plain(weights, lows, highs, norm_train + norm_step)
     *serve, norm = gathered(
-        n, tp, rows, weights, [low.T for low in lows], highs, norm_new.reshape(1, -1)
+        n, tp, rows, weights, [low.T for low in lows], highs, norm_train, norm_step
     )
     return (*flushed(serve), norm.reshape(-1))
 

time: 272 us -> 271 us (level)
  no operation moved by 1% of the time
where the time goes in v3:
time: 271 us; the launch traced here: 266 us
  Pallas kernels  265 us (98%)
    pallas_call x1, Pallas kernels, gathered(): pl.pallas_call(functools.partial(gather_kernel, n, tp, rows), out_shape=[...  259 us
    pallas_call x1, Pallas kernels, flushed(): pl.pallas_call(functools.partial(flush_kernel, len(held)), out_shape=[jax...  5.76 us

profile of v3, /device:TPU:16, one launch (start us, length us, event | category | flops | bytes accessed | tf_op | source)
XLA Modules:
  0.0 266.0 jit_solution(7448410006428014786)
XLA Ops:
  0.6 258.8 %shard_map.138 = (bf16[2048,2560]{1,0:T(8,128)(2,1)S(1)}, bf16[512,2560]{1,0:T(8,128)(2,1)S(1)}, bf16[512,2560]{1,0:T(8,128)(2,1)S(1)}, bf16[8,1,320]{2,1,0:T(2,128)(2,1)}) custom-call(bf16[640,2048]{1,0:T(8,128)(2,1)} %refs_0_.1, bf16[640,512]{1,0:T(8,128)(2,1)} %refs_1_.1, bf16[640,512]{1,0:T(8,128)(2,1)} %refs_2_.1, bf16[64,640]{1,0:T(8,128)(2,1)} %bitcast.3, ...), custom_call_target="tpu_custom_call" | custom-call | tf_op jit(solution)/shard_map/pallas_call | solution.py:169
  259.5 0.0 copy-start
  259.5 5.8 %shard_map.139 = (bf16[2048,2560]{1,0:T(8,128)(2,1)}, bf16[512,2560]{1,0:T(8,128)(2,1)}, bf16[512,2560]{1,0:T(8,128)(2,1)}) custom-call(bf16[2048,2560]{1,0:T(8,128)(2,1)S(1)} %get-tuple-element.11.refs_0_, bf16[512,2560]{1,0:T(8,128)(2,1)S(1)} %get-tuple-element.12.refs_1_, bf16[512,2560]{1,0:T(8,128)(2,1)S(1)} %get-tuple-element.13.refs_2_), custom_call_target="tpu_custom_call" | custom-call | tf_op jit(solution)/shard_map/pallas_call | solution.py:206
  265.2 0.0 copy-done
  265.3 0.7 reshape.11
  (1 shorter events, 0.0 us)
Async XLA Ops:
  259.5 5.8 %copy-start = (bf16[8,1,320]{2,1,0:T(2,128)(2,1)S(1)}, bf16[8,1,320]{2,1,0:T(2,128)(2,1)}, u32[]{:S(2)}) copy-start(bf16[8,1,320]{2,1,0:T(2,128)(2,1)} %get-tuple-element.17) | copy-start | bytes 15364
